TPU v7x, 32 devices: a whole 2x2x4 slice. The times are simulated.
32 devices in a mesh: gx: 8 (over z, x), gy: 4 (over y, core).
Axes of the slice: x: 2, y: 2, z: 4, core: 2. Of those that a mesh axis runs over, the one named last changes fastest.
Arguments:
- velocity: float32 [3, 64, 256, 256], P(None, 'gx', 'gy'), may hold values from -10 to 10
Outputs:
- coefficient: float32 [256], P('gy')
- viscosity: float32 [64, 256, 256], P('gx', 'gy')
All inputs are finite; a program needn't handle non-finite values.
Results may differ from a plain program's by a relative error of at most 0.00002.
Values sent between devices are 32-bit elements; how exact they have to be, the bound alone decides.
A program may use at most 64 MiB of HBM per device.

v0:
```python
import jax
import jax.numpy as jnp
from jax import lax
from jax.sharding import PartitionSpec as P

step_stream = 2.0
step_wall = 0.5
step_span = 1.0
clip_high = 0.1
weights = (1.0, 1.0, 1.0, 2.0, 2.0, 2.0)
index_pairs = ((0, 0), (1, 1), (2, 2), (0, 1), (0, 2), (1, 2))


def padded_2(cells, sides, width, closed):
    for axis, dim in sides:
        count = lax.axis_size(axis)
        ends = count if closed else count - 1
        head = lax.slice_in_dim(cells, 0, width, axis=dim)
        tail = lax.slice_in_dim(cells, cells.shape[dim] - width, cells.shape[dim], axis=dim)
        cells = jnp.concatenate(
            [
                lax.ppermute(tail, axis, [(i, (i + 1) % count) for i in range(ends)]),
                cells,
                lax.ppermute(head, axis, [((i + 1) % count, i) for i in range(ends)]),
            ],
            axis=dim,
        )
    return cells


def strain_inner(padded):
    grad_stream = (padded[:, 2:, 1:-1] - padded[:, :-2, 1:-1]) * (0.5 / step_stream)
    grad_wall = (padded[:, 1:-1, 2:] - padded[:, 1:-1, :-2]) * (0.5 / step_wall)
    centre = padded[:, 1:-1, 1:-1]
    grad_span = (jnp.roll(centre, -1, 3) - jnp.roll(centre, 1, 3)) * (0.5 / step_span)
    gradients = (grad_stream, grad_wall, grad_span)
    return jnp.stack(
        [
            0.5 * (gradients[second][first] + gradients[first][second])
            for first, second in index_pairs
        ]
    )


def weight_column():
    return jnp.asarray(weights, jnp.float32).reshape(6, 1, 1, 1)


def magnitude(strain):
    return jnp.sqrt(2.0 * jnp.sum(weight_column() * strain * strain, axis=0))


def test_filter(field):
    smoothed = 0.25 * field[:, :-2] + 0.5 * field[:, 1:-1] + 0.25 * field[:, 2:]
    return 0.25 * jnp.roll(smoothed, 1, 3) + 0.5 * smoothed + 0.25 * jnp.roll(smoothed, -1, 3)


def plane_sums(velocity_pad, stress_pad, filtered_pad):
    strain_hat = strain_inner(filtered_pad)
    magnitude_hat = magnitude(strain_hat)
    row_values = velocity_pad[:, :, 1:-1]
    products = jnp.stack([row_values[first] * row_values[second] for first, second in index_pairs])
    product_hat = test_filter(products)
    centre = filtered_pad[:, 1:-1, 1:-1]
    leonard = product_hat - jnp.stack(
        [centre[first] * centre[second] for first, second in index_pairs]
    )
    trace_third = (leonard[0] + leonard[1] + leonard[2]) / 3.0
    leonard = jnp.concatenate([leonard[:3] - trace_third[None], leonard[3:]])
    model_tensor = 2.0 * (test_filter(stress_pad) - 4.0 * magnitude_hat[None] * strain_hat)
    numerator = jnp.sum(weight_column() * leonard * model_tensor, axis=(0, 1, 3))
    denominator = jnp.sum(weight_column() * model_tensor * model_tensor, axis=(0, 1, 3))
    return (numerator, denominator)


def local(velocity):
    wall_count = lax.axis_size("gy")
    wall_index = lax.axis_index("gy")
    padded = padded_2(velocity, (("gx", 1), ("gy", 2)), 2, True)
    row_ids = jnp.arange(padded.shape[2])
    interior = padded.shape[2] - 2 * 2
    low_wall = jnp.logical_and(wall_index == 0, row_ids < 2)
    high_wall = jnp.logical_and(wall_index == wall_count - 1, row_ids >= interior + 2)
    inside = jnp.logical_not(jnp.logical_or(low_wall, high_wall))
    wide_pad = jnp.where(inside[None, None, :, None], padded, 0.0)
    velocity_pad = wide_pad[:, 1:-1, 1:-1]
    strain_wide = strain_inner(wide_pad)
    strength_wide = magnitude(strain_wide)
    stress_pad = (strength_wide[None] * strain_wide)[:, :, 1:-1]
    strength = strength_wide[1:-1, 1:-1]
    filtered_pad = test_filter(wide_pad[:, :, 1:-1])
    numerator, denominator = plane_sums(velocity_pad, stress_pad, filtered_pad)
    numerator, denominator = lax.psum((numerator, denominator), "gx")
    raw_profile = jnp.clip(numerator / denominator, 0.0, clip_high)
    rim_values = padded_2(raw_profile, (("gy", 0),), 1, False)
    bottom = jnp.where(wall_index == 0, raw_profile[0], rim_values[0])
    top_edge = jnp.where(wall_index == wall_count - 1, raw_profile[-1], rim_values[-1])
    below_values = jnp.concatenate([bottom[None], raw_profile[:-1]])
    above_values = jnp.concatenate([raw_profile[1:], top_edge[None]])
    smooth = 0.25 * below_values + 0.5 * raw_profile + 0.25 * above_values
    return (smooth, smooth[None, :, None] * strength)


def solution(mesh):
    in_specs = (P(None, "gx", "gy", None),)
    out_specs = (P("gy"), P("gx", "gy", None))
    return jax.shard_map(local, mesh=mesh, in_specs=in_specs, out_specs=out_specs, check_vma=False)
```

profile of v0, /device:TPU:0, one launch (start us, length us, event | category | flops | bytes accessed | tf_op | source)
XLA Modules:
  0.0 102.6 jit_solution(11081968702126409254)
XLA Ops:
  0.6 1.3 %fusion.60 = (f32[3,2,64,256]{3,2,1,0:T(8,128)S(1)}, f32[3,2,64,256]{3,2,1,0:T(8,128)S(1)}) fusion(f32[3,8,64,256]{3,2,1,0:T(8,128)} %param.5), kind=kLoop, calls=%fused_computation.122 | loop fusion | bytes 1572864 | tf_op jit(solution)/shard_map/slice | solution.py:18
  2.0 3.0 %collective-permute-start = (f32[3,2,64,256]{3,2,1,0:T(8,128)S(1)}, f32[3,2,64,256]{3,2,1,0:T(8,128)S(1)}, u32[]{:S(2)}, u32[]{:S(2)}) collective-permute-start(f32[3,2,64,256]{3,2,1,0:T(8,128)S(1)} %get-tuple-element.36), channel_id=1, source_target_pairs={{0,4},{4,8},{8,12},{12,16},{16,20},{20,24},{24,28},{28,0},{1,5},{5... | collective-permute-start | bytes 1179656 | tf_op jit(solution)/shard_map/ppermute | solution.py:22
  5.0 3.1 %collective-permute-start.1 = (f32[3,2,64,256]{3,2,1,0:T(8,128)S(1)}, f32[3,2,64,256]{3,2,1,0:T(8,128)S(1)}, u32[]{:S(2)}, u32[]{:S(2)}) collective-permute-start(f32[3,2,64,256]{3,2,1,0:T(8,128)S(1)} %get-tuple-element.35), channel_id=1, source_target_pairs={{4,0},{8,4},{12,8},{16,12},{20,16},{24,20},{28,24},{0,28},{5,1},{9... | collective-permute-start | bytes 1179656 | tf_op jit(solution)/shard_map/ppermute | solution.py:24
  8.1 13.7 %collective-permute-done = f32[3,2,64,256]{3,2,1,0:T(8,128)S(1)} collective-permute-done((f32[3,2,64,256]{3,2,1,0:T(8,128)S(1)}, f32[3,2,64,256]{3,2,1,0:T(8,128)S(1)}, u32[]{:S(2)}, u32[]{:S(2)}) %collective-permute-start) | collective-permute-done | bytes 393248 | tf_op jit(solution)/shard_map/ppermute | solution.py:22
  22.0 2.0 %collective-permute-done.1 = f32[3,2,64,256]{3,2,1,0:T(8,128)S(1)} collective-permute-done((f32[3,2,64,256]{3,2,1,0:T(8,128)S(1)}, f32[3,2,64,256]{3,2,1,0:T(8,128)S(1)}, u32[]{:S(2)}, u32[]{:S(2)}) %collective-permute-start.1) | collective-permute-done | bytes 393248 | tf_op jit(solution)/shard_map/ppermute | solution.py:24
  24.6 1.5 %collective-permute-done.3 = f32[3,12,2,256]{3,2,1,0:T(2,128)S(1)} collective-permute-done((f32[3,12,2,256]{3,2,1,0:T(2,128)S(1)}, f32[3,12,2,256]{3,2,1,0:T(2,128)S(1)}, u32[]{:S(2)}, u32[]{:S(2)}) %collective-permute-start.3) | collective-permute-done | bytes 73760 | tf_op jit(solution)/shard_map/ppermute | solution.py:24
  26.1 2.6 %collective-permute-done.2 = f32[3,12,2,256]{3,2,1,0:T(2,128)S(1)} collective-permute-done((f32[3,12,2,256]{3,2,1,0:T(2,128)S(1)}, f32[3,12,2,256]{3,2,1,0:T(2,128)S(1)}, u32[]{:S(2)}, u32[]{:S(2)}) %collective-permute-start.2) | collective-permute-done | bytes 73760 | tf_op jit(solution)/shard_map/ppermute | solution.py:22
  30.7 1.4 %fusion.59 = (f32[3,10,66,1]{3,2,1,0:T(8,128)S(1)}, f32[3,10,66,1]{3,2,1,0:T(8,128)}) fusion(f32[3,10,66,256]{3,2,1,0:T(8,128)S(1)} %get-tuple-element.16), kind=kLoop, calls=%fused_computation.121 | loop fusion | bytes 31680 | tf_op jit(solution)/shard_map/jit(_roll_static)/slice | solution.py:55
  33.2 1.2 %fusion.49 = (f32[6,8,64,255]{3,2,1,0:T(8,128)S(1)}, f32[6,8,64,255]{3,2,1,0:T(8,128)S(1)}) fusion(f32[6,8,64,256]{3,2,1,0:T(8,128)S(1)} %fusion.4), kind=kLoop, calls=%fused_computation.111 | loop fusion | bytes 12533760 | tf_op jit(solution)/shard_map/jit(_roll_static)/slice | solution.py:55
  34.4 2.3 %fusion.50 = (f32[6,8,64,1]{3,2,1,0:T(8,128)}, f32[6,8,64,1]{3,2,1,0:T(8,128)}) fusion(f32[6,8,64,256]{3,2,1,0:T(8,128)S(1)} %fusion.4), kind=kLoop, calls=%fused_computation.112 | loop fusion | bytes 49152 | tf_op jit(solution)/shard_map/jit(_roll_static)/slice | solution.py:55
  36.7 2.6 %fusion.17 = f32[3,10,66,256]{3,2,1,0:T(8,128)S(1)} fusion(f32[3,10,66,255]{3,2,1,0:T(8,128)S(1)} %get-tuple-element.32, f32[3,10,66,1]{3,2,1,0:T(8,128)} %get-tuple-element.34, f32[3,10,66,1]{3,2,1,0:T(8,128)S(1)} %get-tuple-element.33, f32[3,10,66,255]{3,2,1,0:T(8,128)S(1)} %get-tuple-element.31, f32[3,10,66,256]{3,2,1,0:T(8,128)S(1)} %get-tuple-element.16), kind=kLoop, calls=%fused_computation.35 | loop fusion | flops 3548160 | bytes 8110080 | tf_op jit(solution)/shard_map/add | solution.py:55
  40.1 2.2 %fusion.57 = (f32[3,8,64,255]{3,2,1,0:T(8,128)}, f32[3,8,64,255]{3,2,1,0:T(8,128)}) fusion(f32[3,10,66,256]{3,2,1,0:T(8,128)S(1)} %fusion.17), kind=kLoop, calls=%fused_computation.119 | loop fusion | bytes 6266880 | tf_op jit(solution)/shard_map/jit(_roll_static)/slice | solution.py:35
  42.3 1.4 %fusion.56 = (f32[3,8,64,1]{3,2,1,0:T(8,128)}, f32[3,8,64,1]{3,2,1,0:T(8,128)}) fusion(f32[3,10,66,256]{3,2,1,0:T(8,128)S(1)} %fusion.17), kind=kLoop, calls=%fused_computation.118 | loop fusion | bytes 24576 | tf_op jit(solution)/shard_map/jit(_roll_static)/slice | solution.py:35
  49.1 1.8 %fusion.52 = (f32[6,8,64,1]{3,2,1,0:T(8,128)S(1)}, f32[6,8,64,1]{3,2,1,0:T(8,128)}) fusion(f32[6,8,64,256]{3,2,1,0:T(8,128)S(1)} %fusion.2), kind=kLoop, calls=%fused_computation.114 | loop fusion | bytes 49152 | tf_op jit(solution)/shard_map/jit(_roll_static)/slice | solution.py:55
  50.9 3.0 %fusion.51 = (f32[6,8,64,255]{3,2,1,0:T(8,128)S(1)}, f32[6,8,64,255]{3,2,1,0:T(8,128)}) fusion(f32[6,8,64,256]{3,2,1,0:T(8,128)S(1)} %fusion.2), kind=kLoop, calls=%fused_computation.113 | loop fusion | bytes 12533760 | tf_op jit(solution)/shard_map/jit(_roll_static)/slice | solution.py:55
  58.3 3.8 %fusion.8 = f32[6,8,64,256]{3,2,1,0:T(8,128)S(1)} fusion(f32[6,8,64,256]{3,2,1,0:T(8,128)} %multiply_dynamic-update-slice_fusion.6, f32[6,8,64,255]{3,2,1,0:T(8,128)S(1)} %get-tuple-element.9, f32[6,8,64,1]{3,2,1,0:T(8,128)S(1)} %copy-done.2, f32[6,8,64,1]{3,2,1,0:T(8,128)S(1)} %copy-done.1, f32[6,8,64,255]{3,2,1,0:T(8,128)S(1)} %get-tuple-element.8, ...), kind=kLoop, calls=%fused_computation.17 | loop fusion | flops 10223616 | bytes 22020096 | tf_op jit(solution)/shard_map/sub | solution.py:65
  62.6 1.0 copy-done.4
  64.1 2.5 %slice_subtract_fusion.1 = (f32[3,8,64,256]{3,2,1,0:T(8,128)S(1)}, f32[3,8,64,256]{3,2,1,0:T(8,128)S(1)}, f32[3,8,64,256]{3,2,1,0:T(8,128)S(1)}) fusion(f32[3,10,66,256]{3,2,1,0:T(8,128)S(1)} %fusion.17, f32[3,8,64,255]{3,2,1,0:T(8,128)S(1)} %copy-done.4, f32[3,8,64,1]{3,2,1,0:T(8,128)} %get-tuple-element.25, f32[3,8,64,1]{3,2,1,0:T(8,128)} %get-tuple-element.26, ...), kind=kLoop, calls=%fused_computation.41 | loop fusion | flops 2752512 | bytes 14155776 | tf_op jit(solution)/shard_map/sub | solution.py:33
  67.7 1.2 %copy-done = f32[6,8,64,255]{3,2,1,0:T(8,128)S(1)} copy-done((f32[6,8,64,255]{3,2,1,0:T(8,128)S(1)}, f32[6,8,64,255]{3,2,1,0:T(8,128)}, u32[]{:S(2)}) %copy-start) | copy-done | bytes 3133464
  69.3 4.1 %multiply_reduce_fusion = (f32[64]{0:T(128)S(1)}, f32[64]{0:T(128)S(1)}) fusion(f32[6]{0:T(128)S(1)} %copy-done.11, f32[3,8,64,256]{3,2,1,0:T(8,128)S(1)} %get-tuple-element.7, f32[3,8,64,256]{3,2,1,0:T(8,128)S(1)} %get-tuple-element.6, f32[6]{0:T(128)S(1)} %copy-done.9, f32[6,8,64,256]{3,2,1,0:T(8,128)S(1)} %fusion.34, ...), kind=kLoop, calls=%fused_computation.27 | loop fusion | flops 17301376 | bytes 22544944 | tf_op jit(solution)/shard_map/reduce_sum | solution.py:72
  73.4 20.7 %all-reduce = (f32[64]{0:T(128)S(1)}, f32[64]{0:T(128)S(1)}) all-reduce(f32[64]{0:T(128)S(1)} %get-tuple-element.3, f32[64]{0:T(128)S(1)} %get-tuple-element.2), channel_id=1, replica_groups=mesh['gx'=8,'gy'=4] {'gx'}, use_global_device_ids=true, to_apply=%region_3.4 | all-reduce | flops 128 | bytes 1024 | tf_op jit(solution)/shard_map/psum | solution.py:93
  94.8 1.8 %collective-permute-start.4 = (f32[1]{0:T(128)}, f32[1]{0:T(128)}, u32[]{:S(2)}, u32[]{:S(2)}) collective-permute-start(f32[1]{0:T(128)} %get-tuple-element.39), channel_id=1, source_target_pairs={{0,1},{1,2},{2,3},{4,5},{5,6},{6,7},{8,9},{9,10},{10,11},{12,13},{... | collective-permute-start | bytes 20 | tf_op jit(solution)/shard_map/ppermute | solution.py:22
  96.6 1.3 %collective-permute-start.5 = (f32[1]{0:T(128)}, f32[1]{0:T(128)}, u32[]{:S(2)}, u32[]{:S(2)}) collective-permute-start(f32[1]{0:T(128)} %get-tuple-element.40), channel_id=1, source_target_pairs={{1,0},{2,1},{3,2},{5,4},{6,5},{7,6},{9,8},{10,9},{11,10},{13,12},{... | collective-permute-start | bytes 20 | tf_op jit(solution)/shard_map/ppermute | solution.py:24
  99.2 1.2 %collective-permute-done.5 = f32[1]{0:T(128)} collective-permute-done((f32[1]{0:T(128)}, f32[1]{0:T(128)}, u32[]{:S(2)}, u32[]{:S(2)}) %collective-permute-start.5) | collective-permute-done | bytes 36 | tf_op jit(solution)/shard_map/ppermute | solution.py:24
  (74 shorter events, 18.5 us)
Async XLA Ops:
  0.6 21.2 %copy-start.8 = (f32[3,8,64,256]{3,2,1,0:T(8,128)S(1)}, f32[3,8,64,256]{3,2,1,0:T(8,128)}, u32[]{:S(2)}) copy-start(f32[3,8,64,256]{3,2,1,0:T(8,128)} %param.5) | copy-start | bytes 4718596
  2.0 19.8 %collective-permute-start = (f32[3,2,64,256]{3,2,1,0:T(8,128)S(1)}, f32[3,2,64,256]{3,2,1,0:T(8,128)S(1)}, u32[]{:S(2)}, u32[]{:S(2)}) collective-permute-start(f32[3,2,64,256]{3,2,1,0:T(8,128)S(1)} %get-tuple-element.36), channel_id=1, source_target_pairs={{0,4},{4,8},{8,12},{12,16},{16,20},{20,24},{24,28},{28,0},{1,5},{5... | collective-permute-start | bytes 1179656 | tf_op jit(solution)/shard_map/ppermute | solution.py:22
  5.0 19.0 %collective-permute-start.1 = (f32[3,2,64,256]{3,2,1,0:T(8,128)S(1)}, f32[3,2,64,256]{3,2,1,0:T(8,128)S(1)}, u32[]{:S(2)}, u32[]{:S(2)}) collective-permute-start(f32[3,2,64,256]{3,2,1,0:T(8,128)S(1)} %get-tuple-element.35), channel_id=1, source_target_pairs={{4,0},{8,4},{12,8},{16,12},{20,16},{24,20},{28,24},{0,28},{5,1},{9... | collective-permute-start | bytes 1179656 | tf_op jit(solution)/shard_map/ppermute | solution.py:24
  24.1 2.0 %collective-permute-start.3 = (f32[3,12,2,256]{3,2,1,0:T(2,128)S(1)}, f32[3,12,2,256]{3,2,1,0:T(2,128)S(1)}, u32[]{:S(2)}, u32[]{:S(2)}) collective-permute-start(f32[3,12,2,256]{3,2,1,0:T(2,128)S(1)} %get-tuple-element.24), channel_id=1, source_target_pairs={{1,0},{2,1},{3,2},{0,3},{5,4},{6,5},{7,6},{4,7},{9,8},{10,9},{11,1... | collective-permute-start | bytes 221192 | tf_op jit(solution)/shard_map/ppermute | solution.py:24
  24.1 4.6 %collective-permute-start.2 = (f32[3,12,2,256]{3,2,1,0:T(2,128)S(1)}, f32[3,12,2,256]{3,2,1,0:T(2,128)S(1)}, u32[]{:S(2)}, u32[]{:S(2)}) collective-permute-start(f32[3,12,2,256]{3,2,1,0:T(2,128)S(1)} %get-tuple-element.23), channel_id=1, source_target_pairs={{0,1},{1,2},{2,3},{3,0},{4,5},{5,6},{6,7},{7,4},{8,9},{9,10},{10,1... | collective-permute-start | bytes 221192 | tf_op jit(solution)/shard_map/ppermute | solution.py:22
  46.1 0.7 copy-start.9
  47.5 0.9 copy-start.6
  54.7 3.5 %copy-start.1 = (f32[6,8,64,1]{3,2,1,0:T(8,128)S(1)}, f32[6,8,64,1]{3,2,1,0:T(8,128)}, u32[]{:S(2)}) copy-start(f32[6,8,64,1]{3,2,1,0:T(8,128)} %get-tuple-element.10) | copy-start | bytes 36868
  54.7 3.5 %copy-start.2 = (f32[6,8,64,1]{3,2,1,0:T(8,128)S(1)}, f32[6,8,64,1]{3,2,1,0:T(8,128)}, u32[]{:S(2)}) copy-start(f32[6,8,64,1]{3,2,1,0:T(8,128)} %get-tuple-element.11) | copy-start | bytes 36868
  62.2 1.4 %copy-start.4 = (f32[3,8,64,255]{3,2,1,0:T(8,128)S(1)}, f32[3,8,64,255]{3,2,1,0:T(8,128)}, u32[]{:S(2)}) copy-start(f32[3,8,64,255]{3,2,1,0:T(8,128)} %get-tuple-element.27) | copy-start | bytes 4700164
  62.2 1.9 %copy-start.5 = (f32[3,8,64,255]{3,2,1,0:T(8,128)S(1)}, f32[3,8,64,255]{3,2,1,0:T(8,128)}, u32[]{:S(2)}) copy-start(f32[3,8,64,255]{3,2,1,0:T(8,128)} %get-tuple-element.28) | copy-start | bytes 4700164
  66.9 1.9 %copy-start = (f32[6,8,64,255]{3,2,1,0:T(8,128)S(1)}, f32[6,8,64,255]{3,2,1,0:T(8,128)}, u32[]{:S(2)}) copy-start(f32[6,8,64,255]{3,2,1,0:T(8,128)} %get-tuple-element.13) | copy-start | bytes 9400324
  66.9 2.3 %copy-start.3 = (f32[6,8,64,1]{3,2,1,0:T(8,128)S(1)}, f32[6,8,64,1]{3,2,1,0:T(8,128)}, u32[]{:S(2)}) copy-start(f32[6,8,64,1]{3,2,1,0:T(8,128)} %get-tuple-element.15) | copy-start | bytes 36868
  67.0 2.3 %copy-start.11 = (f32[6]{0:T(128)S(1)}, f32[6]{0:T(128)}, u32[]{:S(2)}) copy-start(f32[6]{0:T(128)} %constant.5) | copy-start | bytes 76
  69.3 32.4 %copy-start.7 = (f32[10,66,256]{2,1,0:T(8,128)S(1)}, f32[10,66,256]{2,1,0:T(8,128)}, u32[]{:S(2)}) copy-start(f32[10,66,256]{2,1,0:T(8,128)} %copy-done.6) | copy-start | bytes 2027524
  94.8 3.1 %collective-permute-start.4 = (f32[1]{0:T(128)}, f32[1]{0:T(128)}, u32[]{:S(2)}, u32[]{:S(2)}) collective-permute-start(f32[1]{0:T(128)} %get-tuple-element.39), channel_id=1, source_target_pairs={{0,1},{1,2},{2,3},{4,5},{5,6},{6,7},{8,9},{9,10},{10,11},{12,13},{... | collective-permute-start | bytes 20 | tf_op jit(solution)/shard_map/ppermute | solution.py:22
  96.6 3.7 %collective-permute-start.5 = (f32[1]{0:T(128)}, f32[1]{0:T(128)}, u32[]{:S(2)}, u32[]{:S(2)}) collective-permute-start(f32[1]{0:T(128)} %get-tuple-element.40), channel_id=1, source_target_pairs={{1,0},{2,1},{3,2},{5,4},{6,5},{7,6},{9,8},{10,9},{11,10},{13,12},{... | collective-permute-start | bytes 20 | tf_op jit(solution)/shard_map/ppermute | solution.py:24
  101.7 0.9 copy-start.10
where the time goes:
time: 105 us; the launch traced here: 103 us
  other arithmetic  26.2 us (25%)
  local copies, waits for them, and re-layouts  21.4 us (20%)
  waiting for transfers between devices  21 us (20%)
  blocking collectives  20.7 us (20%)
  starting transfers between devices  9.78 us (9%)
  between operations  3.61 us (3%)
    psum x1, blocking collectives, local(): numerator, denominator = lax.psum((numerator, denominator), 'gx')  20.7 us
    ppermute x3, waiting for transfers between devices, padded_2(): lax.ppermute(tail, axis, [(i, (i + 1) % count) for i in range(ends)])  16.3 us
    slice x6, local copies, waits for them, and re-layouts, test_filter(): jnp.roll(smoothed, -1, 3)  10.3 us
    unnamed x20, other arithmetic  5.43 us
    ppermute x3, starting transfers between devices, padded_2(): lax.ppermute(tail, axis, [(i, (i + 1) % count) for i in range(ends)])  5.34 us
    slice x4, local copies, waits for them, and re-layouts, strain_inner(): jnp.roll(centre, 1, 3)  4.79 us
    ppermute x3, waiting for transfers between devices, padded_2(): lax.ppermute(head, axis, [((i + 1) % count, i) for i in range(ends)])  4.63 us
    ppermute x3, starting transfers between devices, padded_2(): lax.ppermute(head, axis, [((i + 1) % count, i) for i in range(ends)])  4.44 us
  transfers between devices with their start and end apart: 6, of which 5 were waited for; matrix products, arithmetic and copies ran while one was open for 0% of the time, Pallas kernels for 0%

commit v1 on v0

v1 whole, which is shorter than its diff:
```python
import functools

import jax
import jax.numpy as jnp
from jax import lax
from jax.experimental import pallas as pl
from jax.experimental.pallas import tpu as pltpu
from jax.sharding import PartitionSpec as P

clip_high = 0.1
pairs = ((0, 0), (1, 1), (2, 2), (0, 1), (0, 2), (1, 2))
MESH = pl.DeviceIdType.MESH
EARLY = 3


def tile(index):
    return pl.ds(pl.multiple_of(index * 8, 8), 8)


def roll_next(value):
    return pltpu.roll(value, value.shape[1] - 1, 1)


def roll_prev(value):
    return pltpu.roll(value, 1, 1)


def filter_span(value):
    pair = value + roll_next(value)
    return pair + roll_prev(pair)


def slope_span(value):
    step = roll_next(value) - value
    return step + roll_prev(step)


def slope_wall(ref, comp, row, t, here):
    rows = lax.broadcasted_iota(jnp.int32, here.shape, 0)
    below = ref[comp, row, tile(t - 1), :]
    above = ref[comp, row, tile(t + 1), :]
    up = pltpu.roll(jnp.where(rows == 0, above, here), 7, 0)
    down = pltpu.roll(jnp.where(rows == 7, below, here), 1, 0)
    return up - down


def strain4(ref, row, t):
    here = [ref[c, row, tile(t), :] for c in range(3)]
    dx = [ref[c, row + 1, tile(t), :] - ref[c, row - 1, tile(t), :] for c in range(3)]
    dy = [slope_wall(ref, c, row, t, here[c]) for c in range(3)]
    dz = [slope_span(here[c]) for c in range(3)]
    s = (
        dx[0],
        4.0 * dy[1],
        2.0 * dz[2],
        2.0 * dy[0] + 0.5 * dx[1],
        dz[0] + 0.5 * dx[2],
        dz[1] + 2.0 * dy[2],
    )
    diag = s[0] * s[0] + s[1] * s[1] + s[2] * s[2]
    off = s[3] * s[3] + s[4] * s[4] + s[5] * s[5]
    return here, s, diag + 2.0 * off


def kernel(n, m, nx, ny, u_hbm, strength_hbm, coef_ref, u, w, v, q, g, strength, accn, accd,
           edge_out, edge_in, mine, gather, own_sem, out_sem, xs_send, xs_recv, ys_send, ys_recv,
           c_send, c_recv, g_send, g_recv):
    nt = ny // 8
    gx = lax.axis_index("gx")
    gy = lax.axis_index("gy")
    left, right = lax.rem(gx + n - 1, n), lax.rem(gx + 1, n)
    not_low, not_high = gy > 0, gy < m - 1
    lanes = mine.shape[-1]

    own = pltpu.make_async_copy(u_hbm, u.at[:, 2:2 + nx, 8:8 + ny, :], own_sem)
    own.start()

    barrier = pltpu.get_barrier_semaphore()

    def greet(i, carry):
        @pl.when(i != gx)
        def _():
            pl.semaphore_signal(barrier, inc=1, device_id=(i, gy), device_id_type=MESH)

        @pl.when(not_low)
        def _():
            pl.semaphore_signal(barrier, inc=1, device_id=(i, gy - 1), device_id_type=MESH)

        @pl.when(not_high)
        def _():
            pl.semaphore_signal(barrier, inc=1, device_id=(i, gy + 1), device_id_type=MESH)

        return carry

    lax.fori_loop(0, n, greet, 0)
    peers = jnp.where(not_low, n, 0) + jnp.where(not_high, n, 0) + (n - 1)
    pl.semaphore_wait(barrier, peers)

    def x_copy(side, t):
        src = 0 if side == 0 else nx - 2
        dst = nx + 2 if side == 0 else 0
        return pltpu.make_async_remote_copy(
            src_ref=u_hbm.at[:, src:src + 2, tile(t - 1), :],
            dst_ref=u.at[:, dst:dst + 2, tile(t), :],
            send_sem=xs_send.at[side, t - 1],
            recv_sem=xs_recv.at[side, t - 1],
            device_id=(left if side == 0 else right, gy),
            device_id_type=MESH,
        )

    def y_copy(side):
        src = 0 if side == 0 else ny - 8
        dst = ny + 8 if side == 0 else 0
        return pltpu.make_async_remote_copy(
            src_ref=u_hbm.at[:, :, src:src + 8, :],
            dst_ref=u.at[:, 2:2 + nx, dst:dst + 8, :],
            send_sem=ys_send.at[side],
            recv_sem=ys_recv.at[side],
            device_id=(gx, gy - 1 if side == 0 else gy + 1),
            device_id_type=MESH,
        )

    def c_copy(side):
        return pltpu.make_async_remote_copy(
            src_ref=edge_out.at[side],
            dst_ref=edge_in.at[side],
            send_sem=c_send.at[side],
            recv_sem=c_recv.at[side],
            device_id=(left if side == 0 else right, gy),
            device_id_type=MESH,
        )

    @pl.when(not_low)
    def _():
        y_copy(0).start()

    @pl.when(not_high)
    def _():
        y_copy(1).start()

    def start_x(t, carry):
        x_copy(0, t).start()
        x_copy(1, t).start()
        return carry

    lax.fori_loop(1, 1 + EARLY, start_x, 0)

    accn[...] = jnp.zeros_like(accn)
    accd[...] = jnp.zeros_like(accd)

    @pl.when(jnp.logical_not(not_low))
    def _():
        u[:, 2:2 + nx, 0:8, :] = jnp.zeros((3, nx, 8, u.shape[3]), jnp.float32)

    @pl.when(jnp.logical_not(not_high))
    def _():
        u[:, 2:2 + nx, ny + 8:ny + 16, :] = jnp.zeros((3, nx, 8, u.shape[3]), jnp.float32)

    @pl.when(not_high)
    def _():
        y_copy(0).wait_recv()

    @pl.when(not_low)
    def _():
        y_copy(1).wait_recv()

    for side in range(2):
        src = 2 if side == 0 else nx
        for c in range(3):
            for r in range(2):
                k = 2 * c + r
                edge_out[side, k:k + 1, :] = u[c, src + r, 7:8, :]
                edge_out[side, 8 + k:9 + k, :] = u[c, src + r, ny + 8:ny + 9, :]
    own.wait()
    for side in range(2):
        c_copy(side).start()
    lax.fori_loop(1 + EARLY, nt + 1, start_x, 0)

    def span_rows(t, rows):
        for c in range(3):
            for row in rows:
                w[c, row, tile(t), :] = filter_span(u[c, row, tile(t), :])

    def filtered_rows(t, rows):
        for c in range(3):
            for row in rows:
                a, b, d = (w[c, row + k, tile(t), :] for k in (-1, 0, 1))
                v[c, row, tile(t), :] = 0.25 * ((a + b) + (b + d))

    def stress_row(t, row, keep):
        here, s, total = strain4(u, row, t)
        size = jnp.sqrt(0.125 * total)
        if keep:
            strength[row - 2, tile(t - 1), :] = size
        for k, (a, b) in enumerate(pairs):
            q[k, row, tile(t - 1), :] = filter_span(here[a] * here[b])
            g[k, row, tile(t - 1), :] = filter_span(size * s[k])

    def sums_row(t, row):
        centre, s, total = strain4(v, row, t)
        scale = jnp.sqrt(2.0 * total)

        def stream(ref, k):
            a, b, d = (ref[k, row + j, tile(t - 1), :] for j in (-1, 0, 1))
            return (a + b) + (b + d)

        leonard = [stream(q, k) - centre[a] * centre[b] for k, (a, b) in enumerate(pairs)]
        third = (leonard[0] + leonard[1] + leonard[2]) * (1.0 / 3.0)
        leonard = [x - third for x in leonard[:3]] + leonard[3:]
        model = [stream(g, k) - scale * s[k] for k in range(6)]
        lm = [x * y for x, y in zip(leonard, model)]
        mm = [x * x for x in model]
        num = (lm[0] + lm[1] + lm[2]) + 2.0 * (lm[3] + lm[4] + lm[5])
        den = (mm[0] + mm[1] + mm[2]) + 2.0 * (mm[3] + mm[4] + mm[5])
        return num, den

    def fold(value):
        parts = [value[:, k:k + 128] for k in range(0, value.shape[1], 128)]
        return functools.reduce(lambda x, y: x + y, parts)

    def sums(t, rows):
        both = [sums_row(t, row) for row in rows]
        num = functools.reduce(lambda x, y: x + y, [b[0] for b in both])
        den = functools.reduce(lambda x, y: x + y, [b[1] for b in both])
        accn[tile(t - 1), :] += fold(num)
        accd[tile(t - 1), :] += fold(den)

    def inner_filter(t, carry):
        span_rows(t, range(2, nx + 2))
        filtered_rows(t, range(3, nx + 1))
        return carry

    lax.fori_loop(0, nt + 2, inner_filter, 0)

    half = (nx - 2) // 2

    def inner_stress(i, carry):
        t = i // half + 1
        row = 3 + 2 * lax.rem(i, half)
        stress_row(t, row, True)
        stress_row(t, row + 1, True)
        return carry

    lax.fori_loop(0, nt * half, inner_stress, 0)

    less = (nx - 4) // 2

    def inner_sums(i, carry):
        t = i // less + 1
        row = 4 + 2 * lax.rem(i, less)
        sums(t, (row, row + 1))
        return carry

    lax.fori_loop(0, nt * less, inner_sums, 0)
    inner_out = pltpu.make_async_copy(
        strength.at[1:nx - 1], strength_hbm.at[1:nx - 1], out_sem.at[0]
    )
    inner_out.start()

    def rim_first(t):
        span_rows(t, (0, 1, nx + 2, nx + 3))
        filtered_rows(t, (1, 2, nx + 1, nx + 2))

    def rim_second(t):
        for row in (1, 2, nx + 1, nx + 2):
            stress_row(t, row, row in (2, nx + 1))
        sums(t, (2, 3, nx, nx + 1))

    def arrive(t, carry):
        x_copy(0, t).wait_recv()
        x_copy(1, t).wait_recv()
        rim_first(t)
        return carry

    lax.fori_loop(1, 1 + EARLY, arrive, 0)
    for side in range(2):
        c_copy(side).wait_recv()
    for side in range(2):
        dst = nx + 2 if side == 0 else 0
        for c in range(3):
            for r in range(2):
                k = 2 * c + r
                u[c, dst + r, 7:8, :] = edge_in[side, k:k + 1, :]
                u[c, dst + r, ny + 8:ny + 9, :] = edge_in[side, 8 + k:9 + k, :]

    def rim_ends(i, carry):
        rim_first(i * (nt + 1))
        return carry

    lax.fori_loop(0, 2, rim_ends, 0)

    def finish(t, carry):
        @pl.when(jnp.logical_and(t > EARLY, t <= nt))
        def _():
            arrive(t, 0)

        rim_second(t - 1)
        return carry

    lax.fori_loop(2, nt + 2, finish, 0)
    rim_out = []
    for k, row in enumerate((0, nx - 1)):
        copy = pltpu.make_async_copy(
            strength.at[row], strength_hbm.at[row], out_sem.at[1 + k]
        )
        copy.start()
        rim_out.append(copy)

    mine[0:1, :] = jnp.sum(accn[...].T, axis=0, keepdims=True)
    mine[1:2, :] = jnp.sum(accd[...].T, axis=0, keepdims=True)

    def g_copy(kind, to_x, to_y, from_x):
        return pltpu.make_async_remote_copy(
            src_ref=mine,
            dst_ref=gather.at[kind, from_x],
            send_sem=g_send.at[kind, to_x],
            recv_sem=g_recv.at[kind, from_x],
            device_id=(to_x, to_y),
            device_id_type=MESH,
        )

    def send(i, carry):
        @pl.when(i != gx)
        def _():
            g_copy(0, i, gy, gx).start()

        @pl.when(not_low)
        def _():
            g_copy(2, i, gy - 1, gx).start()

        @pl.when(not_high)
        def _():
            g_copy(1, i, gy + 1, gx).start()

        return carry

    lax.fori_loop(0, n, send, 0)
    gather[0, gx] = mine[...]

    def take(i, carry):
        @pl.when(i != gx)
        def _():
            g_copy(0, i, gy, i).wait_recv()

        @pl.when(not_low)
        def _():
            g_copy(1, i, gy, i).wait_recv()

        @pl.when(not_high)
        def _():
            g_copy(2, i, gy, i).wait_recv()

        return carry

    lax.fori_loop(0, n, take, 0)

    def profile(kind):
        def add(i, total):
            return total + gather[kind, i]

        total = lax.fori_loop(0, n, add, jnp.zeros((2, lanes), jnp.float32))
        return jnp.clip(2.0 * (total[0:1] / total[1:2]), 0.0, clip_high)

    raw = profile(0)
    where = lax.broadcasted_iota(jnp.int32, (1, lanes), 1)
    first = where == 0
    last = where == ny - 1
    under = jnp.where(first, raw, pltpu.roll(raw, 1, 1))
    over = jnp.where(last, raw, pltpu.roll(raw, lanes - 1, 1))
    low_raw = pltpu.roll(profile(1), (lanes + 1 - ny) % lanes, 1)
    high_raw = pltpu.roll(profile(2), ny - 1, 1)
    under = jnp.where(jnp.logical_and(first, not_low), low_raw, under)
    over = jnp.where(jnp.logical_and(last, not_high), high_raw, over)
    coef_ref[...] = 0.25 * under + 0.5 * raw + 0.25 * over

    def left_x(t, carry):
        x_copy(0, t).wait_send()
        x_copy(1, t).wait_send()
        return carry

    lax.fori_loop(1, nt + 1, left_x, 0)
    for side in range(2):
        c_copy(side).wait_send()

    @pl.when(not_low)
    def _():
        y_copy(0).wait_send()

    @pl.when(not_high)
    def _():
        y_copy(1).wait_send()

    def left_g(i, carry):
        @pl.when(i != gx)
        def _():
            g_copy(0, i, gy, gx).wait_send()

        @pl.when(not_low)
        def _():
            g_copy(2, i, gy - 1, gx).wait_send()

        @pl.when(not_high)
        def _():
            g_copy(1, i, gy + 1, gx).wait_send()

        return carry

    lax.fori_loop(0, n, left_g, 0)
    inner_out.wait()
    for copy in rim_out:
        copy.wait()


def local(n, m, velocity):
    _, nx, ny, nz = velocity.shape
    lanes = -(-ny // 128) * 128
    nt = ny // 8
    f32 = jnp.float32
    strength, coef = pl.pallas_call(
        functools.partial(kernel, n, m, nx, ny),
        out_shape=(
            jax.ShapeDtypeStruct((nx, ny, nz), f32),
            jax.ShapeDtypeStruct((1, lanes), f32),
        ),
        in_specs=[pl.BlockSpec(memory_space=pl.ANY)],
        out_specs=(
            pl.BlockSpec(memory_space=pl.ANY),
            pl.BlockSpec(memory_space=pltpu.VMEM),
        ),
        scratch_shapes=[
            pltpu.VMEM((3, nx + 4, ny + 16, nz), f32),
            pltpu.VMEM((3, nx + 4, ny + 16, nz), f32),
            pltpu.VMEM((3, nx + 4, ny + 16, nz), f32),
            pltpu.VMEM((6, nx + 4, ny, nz), f32),
            pltpu.VMEM((6, nx + 4, ny, nz), f32),
            pltpu.VMEM((nx, ny, nz), f32),
            pltpu.VMEM((lanes, 128), f32),
            pltpu.VMEM((lanes, 128), f32),
            pltpu.VMEM((2, 16, nz), f32),
            pltpu.VMEM((2, 16, nz), f32),
            pltpu.VMEM((2, lanes), f32),
            pltpu.VMEM((3, n, 2, lanes), f32),
            pltpu.SemaphoreType.DMA,
            pltpu.SemaphoreType.DMA((3,)),
            pltpu.SemaphoreType.DMA((2, nt)),
            pltpu.SemaphoreType.DMA((2, nt)),
            pltpu.SemaphoreType.DMA((2,)),
            pltpu.SemaphoreType.DMA((2,)),
            pltpu.SemaphoreType.DMA((2,)),
            pltpu.SemaphoreType.DMA((2,)),
            pltpu.SemaphoreType.DMA((3, n)),
            pltpu.SemaphoreType.DMA((3, n)),
        ],
        compiler_params=pltpu.CompilerParams(
            collective_id=0, has_side_effects=True, vmem_limit_bytes=48 * 1024 * 1024
        ),
    )(velocity)
    smooth = coef[0, :ny]
    return (smooth, smooth[None, :, None] * strength)


def solution(mesh):
    n, m = mesh.shape["gx"], mesh.shape["gy"]
    return jax.shard_map(
        functools.partial(local, n, m),
        mesh=mesh,
        in_specs=(P(None, "gx", "gy", None),),
        out_specs=(P("gy"), P("gx", "gy", None)),
        check_vma=False,
    )
```

time: 105 us -> 41 us (0.39); the launches traced: 103 us -> 40.7 us
  Pallas kernels: 0 us -> 37.7 us
  other arithmetic: 26.2 us -> 0.9 us
  waiting for transfers between devices: 21 us -> 0 us
  blocking collectives: 20.7 us -> 0 us
  local copies, waits for them, and re-layouts: 21.4 us -> 1.41 us
  starting transfers between devices: 9.78 us -> 0 us
  between operations: 3.61 us -> 0.66 us
    pallas_call x0 -> x1, Pallas kernels: none -> 37.7 us  [local(): pl.pallas_call(functools.partial(kernel, n, m, nx, ny), out_shape=(jax.Sh...]
    ppermute x6 -> x0, waiting for transfers between devices: 21 us -> none  [the longest x3 16.3 us: padded_2(): lax.ppermute(tail, axis, [(i, (i + 1) % count) for i in range(ends)])]
    psum x1 -> x0, blocking collectives: 20.7 us -> none  [local(): numerator, denominator = lax.psum((numerator, denominator), 'gx')]
    slice x14 -> x0, local copies, waits for them, and re-layouts: 17.2 us -> none  [the longest x6 10.3 us: test_filter(): jnp.roll(smoothed, -1, 3)]
    ppermute x6 -> x0, starting transfers between devices: 9.78 us -> none  [the longest x3 5.34 us: padded_2(): lax.ppermute(tail, axis, [(i, (i + 1) % count) for i in range(ends)])]
    sub x4 -> x0, other arithmetic: 6.82 us -> none  [the longest x1 3.78 us: plane_sums(): product_hat - jnp.stack([centre[first] * centre[second] for first, second...]
    unnamed x20 -> x0, other arithmetic: 5.43 us -> none
    reduce_sum x3 -> x0, other arithmetic: 5.14 us -> none  [the longest x1 4.14 us: plane_sums(): jnp.sum(weight_column() * model_tensor * model_tensor, axis=(0, 1, 3))]
  transfers between devices with their start and end apart: 6 -> 0, of which waited for: 5 -> 0; matrix products, arithmetic and copies ran while one was open for 0% -> 0% of each run, Pallas kernels for 0% -> 0%
where the time goes in v1:
time: 41 us; the launch traced here: 40.7 us
  Pallas kernels  37.7 us (92%)
  local copies, waits for them, and re-layouts  1.41 us (3%)
  other arithmetic  0.9 us (2%)
  between operations  0.66 us (2%)
    pallas_call x1, Pallas kernels, local(): pl.pallas_call(functools.partial(kernel, n, m, nx, ny), out_shape=(jax.Sh...  37.7 us
    unnamed x4, local copies, waits for them, and re-layouts  1.41 us
    mul x1, other arithmetic, local(): return (smooth, smooth[None, :, None] * strength)  0.9 us

profile of v1, /device:TPU:0, one launch (start us, length us, event | category | flops | bytes accessed | tf_op | source)
XLA Modules:
  0.0 40.7 jit_solution(4419224350193852518)
XLA Ops:
  0.6 0.0 copy-start
  0.6 1.4 %copy-done = f32[3,8,64,256]{3,2,1,0:T(8,128)S(1)} copy-done((f32[3,8,64,256]{3,2,1,0:T(8,128)S(1)}, f32[3,8,64,256]{3,2,1,0:T(8,128)}, u32[]{:S(2)}) %copy-start) | copy-done | bytes 1572888
  2.0 37.7 %shard_map.30 = (f32[8,64,256]{2,1,0:T(8,128)S(1)}, f32[1,128]{1,0:T(1,128)S(1)}) custom-call(f32[3,8,64,256]{3,2,1,0:T(8,128)S(1)} %copy-done), custom_call_target="tpu_custom_call" | custom-call | tf_op jit(solution)/shard_map/pallas_call | solution.py:419
  39.7 0.0 copy-start.1
  39.8 0.9 %broadcast_multiply_fusion = f32[8,64,256]{2,1,0:T(8,128)} fusion(f32[8,64,256]{2,1,0:T(8,128)S(1)} %get-tuple-element.5, f32[64]{0:T(128)S(1)} %slice_bitcast_fusion), kind=kLoop, calls=%fused_computation | loop fusion | flops 131072 | bytes 1048832 | tf_op jit(solution)/shard_map/mul | solution.py:459
  40.7 0.0 copy-done.1
  (1 shorter events, 0.0 us)
Async XLA Ops:
  0.6 1.4 %copy-start = (f32[3,8,64,256]{3,2,1,0:T(8,128)S(1)}, f32[3,8,64,256]{3,2,1,0:T(8,128)}, u32[]{:S(2)}) copy-start(f32[3,8,64,256]{3,2,1,0:T(8,128)} %u_hbm.1) | copy-start | bytes 4718596
  39.7 0.9 %copy-start.1 = (f32[64]{0:T(128)}, f32[64]{0:T(128)S(1)}, u32[]{:S(2)}) copy-start(f32[64]{0:T(128)S(1)} %slice_bitcast_fusion) | copy-start | bytes 772

commit v2 on v1

--- a/solution.py
+++ b/solution.py
@@ -26,13 +26,11 @@
 
 
 def filter_span(value):
-    pair = value + roll_next(value)
-    return pair + roll_prev(pair)
+    return (roll_next(value) + roll_prev(value)) + 2.0 * value
 
 
 def slope_span(value):
-    step = roll_next(value) - value
-    return step + roll_prev(step)
+    return roll_next(value) - roll_prev(value)
 
 
 def slope_wall(ref, comp, row, t, here):
@@ -44,11 +42,14 @@
     return up - down
 
 
-def strain4(ref, row, t):
+def strain4(ref, row, t, slope=None):
     here = [ref[c, row, tile(t), :] for c in range(3)]
     dx = [ref[c, row + 1, tile(t), :] - ref[c, row - 1, tile(t), :] for c in range(3)]
     dy = [slope_wall(ref, c, row, t, here[c]) for c in range(3)]
-    dz = [slope_span(here[c]) for c in range(3)]
+    if slope is None:
+        dz = [slope_span(here[c]) for c in range(3)]
+    else:
+        dz = [slope[c, row, tile(t), :] for c in range(3)]
     s = (
         dx[0],
         4.0 * dy[1],
@@ -62,9 +63,9 @@
     return here, s, diag + 2.0 * off
 
 
-def kernel(n, m, nx, ny, u_hbm, strength_hbm, coef_ref, u, w, v, q, g, strength, accn, accd,
+def kernel(n, m, nx, ny, u_hbm, strength_hbm, coef_ref, u, w, v, d, g, strength, accn, accd,
            edge_out, edge_in, mine, gather, own_sem, out_sem, xs_send, xs_recv, ys_send, ys_recv,
-           c_send, c_recv, g_send, g_recv):
+           c_send, c_recv, g_send, g_recv, ring):
     nt = ny // 8
     gx = lax.axis_index("gx")
     gy = lax.axis_index("gy")
@@ -77,24 +78,33 @@
 
     barrier = pltpu.get_barrier_semaphore()
 
-    def greet(i, carry):
-        @pl.when(i != gx)
-        def _():
-            pl.semaphore_signal(barrier, inc=1, device_id=(i, gy), device_id_type=MESH)
-
+    def to_ends(semaphore):
         @pl.when(not_low)
         def _():
-            pl.semaphore_signal(barrier, inc=1, device_id=(i, gy - 1), device_id_type=MESH)
+            pl.semaphore_signal(semaphore, inc=1, device_id=(gx, gy - 1), device_id_type=MESH)
 
         @pl.when(not_high)
         def _():
-            pl.semaphore_signal(barrier, inc=1, device_id=(i, gy + 1), device_id_type=MESH)
-
-        return carry
-
-    lax.fori_loop(0, n, greet, 0)
-    peers = jnp.where(not_low, n, 0) + jnp.where(not_high, n, 0) + (n - 1)
-    pl.semaphore_wait(barrier, peers)
+            pl.semaphore_signal(semaphore, inc=1, device_id=(gx, gy + 1), device_id_type=MESH)
+
+    def to_sides(semaphore):
+        for side in (left, right):
+            pl.semaphore_signal(semaphore, inc=1, device_id=(side, gy), device_id_type=MESH)
+
+    to_sides(barrier)
+    to_ends(barrier)
+    ends = jnp.where(not_low, 1, 0) + jnp.where(not_high, 1, 0)
+    pl.semaphore_wait(barrier, ends + 2)
+
+    rounds = n // 2 - 1
+
+    def open_round(k):
+        if k < rounds:
+            to_sides(ring.at[k])
+
+    def close_round(k):
+        if k < rounds:
+            pl.semaphore_wait(ring.at[k], 2)
 
     def x_copy(side, t):
         src = 0 if side == 0 else nx - 2
@@ -176,38 +186,46 @@
         c_copy(side).start()
     lax.fori_loop(1 + EARLY, nt + 1, start_x, 0)
 
-    def span_rows(t, rows):
+    def span_rows(t, rows, slopes=True):
         for c in range(3):
             for row in rows:
-                w[c, row, tile(t), :] = filter_span(u[c, row, tile(t), :])
+                here = u[c, row, tile(t), :]
+                after, before = roll_next(here), roll_prev(here)
+                w[c, row, tile(t), :] = (after + before) + 2.0 * here
+                if slopes:
+                    d[c, row, tile(t), :] = after - before
 
     def filtered_rows(t, rows):
         for c in range(3):
             for row in rows:
-                a, b, d = (w[c, row + k, tile(t), :] for k in (-1, 0, 1))
-                v[c, row, tile(t), :] = 0.25 * ((a + b) + (b + d))
+                a, b, e = (w[c, row + k, tile(t), :] for k in (-1, 0, 1))
+                v[c, row, tile(t), :] = 0.25 * ((a + e) + 2.0 * b)
 
     def stress_row(t, row, keep):
-        here, s, total = strain4(u, row, t)
+        _, s, total = strain4(u, row, t, d)
         size = jnp.sqrt(0.125 * total)
         if keep:
             strength[row - 2, tile(t - 1), :] = size
-        for k, (a, b) in enumerate(pairs):
-            q[k, row, tile(t - 1), :] = filter_span(here[a] * here[b])
-            g[k, row, tile(t - 1), :] = filter_span(size * s[k])
+        for k in range(6):
+            g[k, row, tile(t - 1), :] = size * s[k]
 
     def sums_row(t, row):
         centre, s, total = strain4(v, row, t)
         scale = jnp.sqrt(2.0 * total)
 
-        def stream(ref, k):
-            a, b, d = (ref[k, row + j, tile(t - 1), :] for j in (-1, 0, 1))
-            return (a + b) + (b + d)
-
-        leonard = [stream(q, k) - centre[a] * centre[b] for k, (a, b) in enumerate(pairs)]
+        def product(a, b):
+            one, two, three = (near[j][a] * near[j][b] for j in range(3))
+            return filter_span((one + three) + 2.0 * two)
+
+        def stress(k):
+            one, two, three = (g[k, row + j, tile(t - 1), :] for j in (-1, 0, 1))
+            return filter_span((one + three) + 2.0 * two)
+
+        near = [[u[c, row + j, tile(t), :] for c in range(3)] for j in (-1, 0, 1)]
+        leonard = [product(a, b) - centre[a] * centre[b] for a, b in pairs]
         third = (leonard[0] + leonard[1] + leonard[2]) * (1.0 / 3.0)
         leonard = [x - third for x in leonard[:3]] + leonard[3:]
-        model = [stream(g, k) - scale * s[k] for k in range(6)]
+        model = [stress(k) - scale * s[k] for k in range(6)]
         lm = [x * y for x, y in zip(leonard, model)]
         mm = [x * x for x in model]
         num = (lm[0] + lm[1] + lm[2]) + 2.0 * (lm[3] + lm[4] + lm[5])
@@ -225,6 +243,8 @@
         accn[tile(t - 1), :] += fold(num)
         accd[tile(t - 1), :] += fold(den)
 
+    open_round(0)
+
     def inner_filter(t, carry):
         span_rows(t, range(2, nx + 2))
         filtered_rows(t, range(3, nx + 1))
@@ -232,6 +252,8 @@
 
     lax.fori_loop(0, nt + 2, inner_filter, 0)
 
+    close_round(0)
+    open_round(1)
     half = (nx - 2) // 2
 
     def inner_stress(i, carry):
@@ -243,22 +265,32 @@
 
     lax.fori_loop(0, nt * half, inner_stress, 0)
 
-    less = (nx - 4) // 2
-
-    def inner_sums(i, carry):
-        t = i // less + 1
-        row = 4 + 2 * lax.rem(i, less)
-        sums(t, (row, row + 1))
-        return carry
-
-    lax.fori_loop(0, nt * less, inner_sums, 0)
+    close_round(1)
+    open_round(2)
+
+    def inner_sums(t, carry):
+        sums(t, range(4, nx))
+        return carry
+
+    lax.fori_loop(1, nt + 1, inner_sums, 0)
+    close_round(2)
+
+    def later_round(k, carry):
+        to_sides(ring.at[k])
+        pl.semaphore_wait(ring.at[k], 2)
+        return carry
+
+    if rounds > 3:
+        lax.fori_loop(3, rounds, later_round, 0)
+    to_ends(ring.at[n // 2])
     inner_out = pltpu.make_async_copy(
         strength.at[1:nx - 1], strength_hbm.at[1:nx - 1], out_sem.at[0]
     )
     inner_out.start()
 
     def rim_first(t):
-        span_rows(t, (0, 1, nx + 2, nx + 3))
+        span_rows(t, (0, nx + 3), False)
+        span_rows(t, (1, nx + 2))
         filtered_rows(t, (1, 2, nx + 1, nx + 2))
 
     def rim_second(t):
@@ -305,6 +337,8 @@
         )
         copy.start()
         rim_out.append(copy)
+
+    pl.semaphore_wait(ring.at[n // 2], ends)
 
     mine[0:1, :] = jnp.sum(accn[...].T, axis=0, keepdims=True)
     mine[1:2, :] = jnp.sum(accd[...].T, axis=0, keepdims=True)
@@ -431,7 +465,7 @@
             pltpu.VMEM((3, nx + 4, ny + 16, nz), f32),
             pltpu.VMEM((3, nx + 4, ny + 16, nz), f32),
             pltpu.VMEM((3, nx + 4, ny + 16, nz), f32),
-            pltpu.VMEM((6, nx + 4, ny, nz), f32),
+            pltpu.VMEM((3, nx + 4, ny + 16, nz), f32),
             pltpu.VMEM((6, nx + 4, ny, nz), f32),
             pltpu.VMEM((nx, ny, nz), f32),
             pltpu.VMEM((lanes, 128), f32),
@@ -450,9 +484,10 @@
             pltpu.SemaphoreType.DMA((2,)),
             pltpu.SemaphoreType.DMA((3, n)),
             pltpu.SemaphoreType.DMA((3, n)),
+            pltpu.SemaphoreType.REGULAR((n // 2 + 1,)),
         ],
         compiler_params=pltpu.CompilerParams(
-            collective_id=0, has_side_effects=True, vmem_limit_bytes=48 * 1024 * 1024
+            collective_id=0, has_side_effects=True, vmem_limit_bytes=67043328
         ),
     )(velocity)
     smooth = coef[0, :ny]

time: 41 us -> 34.7 us (0.85)
  Pallas kernels: 37.7 us -> 31.3 us
  other arithmetic: 0.9 us -> 1.95 us
  local copies, waits for them, and re-layouts: 1.41 us -> 0.68 us
    pallas_call x1, Pallas kernels: 37.7 us -> 31.3 us  [local(): pl.pallas_call(functools.partial(kernel, n, m, nx, ny), out_shape=(jax.Sh...]
    unnamed x4 -> x2, local copies, waits for them, and re-layouts: 1.41 us -> 0.01 us
    mul x1, other arithmetic: 0.9 us -> 1.95 us  [local(): return (smooth, smooth[None, :, None] * strength)]
    squeeze x1, local copies, waits for them, and re-layouts: 0.01 us -> 0.67 us  [local(): smooth = coef[0, :ny]]
where the time goes in v2:
time: 34.7 us; the launch traced here: 34.5 us
  Pallas kernels  31.3 us (90%)
  other arithmetic  1.95 us (6%)
  local copies, waits for them, and re-layouts  0.68 us (2%)
  between operations  0.64 us (2%)
    pallas_call x1, Pallas kernels, local(): pl.pallas_call(functools.partial(kernel, n, m, nx, ny), out_shape=(jax.Sh...  31.3 us
    mul x1, other arithmetic, local(): return (smooth, smooth[None, :, None] * strength)  1.95 us

profile of v2, /device:TPU:0, one launch (start us, length us, event | category | flops | bytes accessed | tf_op | source)
XLA Modules:
  0.0 34.5 jit_solution(1912289005930923479)
XLA Ops:
  0.6 31.3 %shard_map.30 = (f32[8,64,256]{2,1,0:T(8,128)}, f32[1,128]{1,0:T(1,128)}) custom-call(f32[3,8,64,256]{3,2,1,0:T(8,128)} %u_hbm.1), custom_call_target="tpu_custom_call" | custom-call | tf_op jit(solution)/shard_map/pallas_call | solution.py:453
  31.9 0.7 %slice_bitcast_fusion = f32[64]{0:T(128)S(1)} fusion(f32[1,128]{1,0:T(1,128)} %get-tuple-element.4), kind=kLoop, calls=%fused_computation.1 | loop fusion | bytes 512 | tf_op jit(solution)/shard_map/squeeze | solution.py:493
  32.6 0.0 copy-start
  32.6 1.9 %broadcast_multiply_fusion = f32[8,64,256]{2,1,0:T(8,128)} fusion(f32[8,64,256]{2,1,0:T(8,128)} %get-tuple-element.5, f32[64]{0:T(128)S(1)} %slice_bitcast_fusion), kind=kLoop, calls=%fused_computation | loop fusion | flops 131072 | bytes 1048832 | tf_op jit(solution)/shard_map/mul | solution.py:494
  34.5 0.0 copy-done
Async XLA Ops:
  32.6 1.9 %copy-start = (f32[64]{0:T(128)}, f32[64]{0:T(128)S(1)}, u32[]{:S(2)}) copy-start(f32[64]{0:T(128)S(1)} %slice_bitcast_fusion) | copy-start | bytes 772

commit v3 on v2

--- a/solution.py
+++ b/solution.py
@@ -10,7 +10,7 @@
 clip_high = 0.1
 pairs = ((0, 0), (1, 1), (2, 2), (0, 1), (0, 2), (1, 2))
 MESH = pl.DeviceIdType.MESH
-EARLY = 3
+EARLY = 4
 
 
 def tile(index):
@@ -63,8 +63,8 @@
     return here, s, diag + 2.0 * off
 
 
-def kernel(n, m, nx, ny, u_hbm, strength_hbm, coef_ref, u, w, v, d, g, strength, accn, accd,
-           edge_out, edge_in, mine, gather, own_sem, out_sem, xs_send, xs_recv, ys_send, ys_recv,
+def kernel(n, m, nx, ny, u_hbm, strength, coef_ref, u, w, v, d, g, accn, accd,
+           edge_out, edge_in, mine, mine_ends, gather, own_sem, xs_send, xs_recv, ys_send, ys_recv,
            c_send, c_recv, g_send, g_recv, ring):
     nt = ny // 8
     gx = lax.axis_index("gx")
@@ -95,6 +95,7 @@
     to_ends(barrier)
     ends = jnp.where(not_low, 1, 0) + jnp.where(not_high, 1, 0)
     pl.semaphore_wait(barrier, ends + 2)
+    own.wait()
 
     rounds = n // 2 - 1
 
@@ -107,22 +108,33 @@
             pl.semaphore_wait(ring.at[k], 2)
 
     def x_copy(side, t):
-        src = 0 if side == 0 else nx - 2
+        src = 2 if side == 0 else nx
         dst = nx + 2 if side == 0 else 0
         return pltpu.make_async_remote_copy(
-            src_ref=u_hbm.at[:, src:src + 2, tile(t - 1), :],
+            src_ref=u.at[:, src:src + 2, tile(t), :],
             dst_ref=u.at[:, dst:dst + 2, tile(t), :],
-            send_sem=xs_send.at[side, t - 1],
+            send_sem=xs_send.at[side],
             recv_sem=xs_recv.at[side, t - 1],
             device_id=(left if side == 0 else right, gy),
             device_id_type=MESH,
         )
 
+    def x_all(side):
+        part = u.at[:, 2:4, 8:8 + ny, :]
+        return pltpu.make_async_remote_copy(
+            src_ref=part,
+            dst_ref=part,
+            send_sem=xs_send.at[side],
+            recv_sem=xs_recv.at[side, 0],
+            device_id=(right, gy),
+            device_id_type=MESH,
+        )
+
     def y_copy(side):
-        src = 0 if side == 0 else ny - 8
+        src = 8 if side == 0 else ny
         dst = ny + 8 if side == 0 else 0
         return pltpu.make_async_remote_copy(
-            src_ref=u_hbm.at[:, :, src:src + 8, :],
+            src_ref=u.at[:, 2:2 + nx, src:src + 8, :],
             dst_ref=u.at[:, 2:2 + nx, dst:dst + 8, :],
             send_sem=ys_send.at[side],
             recv_sem=ys_recv.at[side],
@@ -148,12 +160,13 @@
     def _():
         y_copy(1).start()
 
-    def start_x(t, carry):
+    def start_x(i, carry):
+        t = jnp.where(i < 2, nt - i, i - 1)
         x_copy(0, t).start()
         x_copy(1, t).start()
         return carry
 
-    lax.fori_loop(1, 1 + EARLY, start_x, 0)
+    lax.fori_loop(0, EARLY, start_x, 0)
 
     accn[...] = jnp.zeros_like(accn)
     accd[...] = jnp.zeros_like(accd)
@@ -181,10 +194,9 @@
                 k = 2 * c + r
                 edge_out[side, k:k + 1, :] = u[c, src + r, 7:8, :]
                 edge_out[side, 8 + k:9 + k, :] = u[c, src + r, ny + 8:ny + 9, :]
-    own.wait()
     for side in range(2):
         c_copy(side).start()
-    lax.fori_loop(1 + EARLY, nt + 1, start_x, 0)
+    lax.fori_loop(EARLY, nt, start_x, 0)
 
     def span_rows(t, rows, slopes=True):
         for c in range(3):
@@ -283,10 +295,6 @@
     if rounds > 3:
         lax.fori_loop(3, rounds, later_round, 0)
     to_ends(ring.at[n // 2])
-    inner_out = pltpu.make_async_copy(
-        strength.at[1:nx - 1], strength_hbm.at[1:nx - 1], out_sem.at[0]
-    )
-    inner_out.start()
 
     def rim_first(t):
         span_rows(t, (0, nx + 3), False)
@@ -298,13 +306,16 @@
             stress_row(t, row, row in (2, nx + 1))
         sums(t, (2, 3, nx, nx + 1))
 
-    def arrive(t, carry):
+    def arrive(t):
         x_copy(0, t).wait_recv()
         x_copy(1, t).wait_recv()
         rim_first(t)
-        return carry
-
-    lax.fori_loop(1, 1 + EARLY, arrive, 0)
+
+    def arrive_early(i, carry):
+        arrive(jnp.where(i < 2, nt - i, i - 1))
+        return carry
+
+    lax.fori_loop(0, EARLY, arrive_early, 0)
     for side in range(2):
         c_copy(side).wait_recv()
     for side in range(2):
@@ -321,72 +332,81 @@
 
     lax.fori_loop(0, 2, rim_ends, 0)
 
-    def finish(t, carry):
-        @pl.when(jnp.logical_and(t > EARLY, t <= nt))
-        def _():
-            arrive(t, 0)
-
-        rim_second(t - 1)
-        return carry
-
-    lax.fori_loop(2, nt + 2, finish, 0)
-    rim_out = []
-    for k, row in enumerate((0, nx - 1)):
-        copy = pltpu.make_async_copy(
-            strength.at[row], strength_hbm.at[row], out_sem.at[1 + k]
-        )
-        copy.start()
-        rim_out.append(copy)
-
-    pl.semaphore_wait(ring.at[n // 2], ends)
-
-    mine[0:1, :] = jnp.sum(accn[...].T, axis=0, keepdims=True)
-    mine[1:2, :] = jnp.sum(accd[...].T, axis=0, keepdims=True)
-
-    def g_copy(kind, to_x, to_y, from_x):
+    def finish_ends(i, carry):
+        rim_second(1 + i * (nt - 1))
+        return carry
+
+    lax.fori_loop(0, 2, finish_ends, 0)
+
+    def column_sums(ref):
+        ref[0:1, :] = jnp.sum(accn[...].T, axis=0, keepdims=True)
+        ref[1:2, :] = jnp.sum(accd[...].T, axis=0, keepdims=True)
+
+    def g_copy(kind, to_x, to_y):
         return pltpu.make_async_remote_copy(
-            src_ref=mine,
-            dst_ref=gather.at[kind, from_x],
-            send_sem=g_send.at[kind, to_x],
-            recv_sem=g_recv.at[kind, from_x],
+            src_ref=mine if kind == 0 else mine_ends,
+            dst_ref=gather.at[kind, gx],
+            send_sem=g_send.at[kind],
+            recv_sem=g_recv.at[kind],
             device_id=(to_x, to_y),
             device_id_type=MESH,
         )
 
-    def send(i, carry):
-        @pl.when(i != gx)
-        def _():
-            g_copy(0, i, gy, gx).start()
-
+    def g_all(kind):
+        count = n - 1 if kind == 0 else n
+        part = gather.at[kind, 0:count]
+        return pltpu.make_async_remote_copy(
+            src_ref=part,
+            dst_ref=part,
+            send_sem=g_send.at[kind],
+            recv_sem=g_recv.at[kind],
+            device_id=(right, gy),
+            device_id_type=MESH,
+        )
+
+    column_sums(mine_ends)
+    pl.semaphore_wait(ring.at[n // 2], ends)
+
+    def send_ends(i, carry):
         @pl.when(not_low)
         def _():
-            g_copy(2, i, gy - 1, gx).start()
+            g_copy(2, i, gy - 1).start()
 
         @pl.when(not_high)
         def _():
-            g_copy(1, i, gy + 1, gx).start()
-
-        return carry
-
-    lax.fori_loop(0, n, send, 0)
+            g_copy(1, i, gy + 1).start()
+
+        return carry
+
+    lax.fori_loop(0, n, send_ends, 0)
+
+    def finish(t, carry):
+        @pl.when(t < nt - 1)
+        def _():
+            arrive(t)
+
+        rim_second(t - 1)
+        return carry
+
+    lax.fori_loop(EARLY - 1, nt + 1, finish, 0)
+
+    column_sums(mine)
+
+    def send(i, carry):
+        g_copy(0, lax.rem(gx + i, n), gy).start()
+        return carry
+
+    lax.fori_loop(1, n, send, 0)
     gather[0, gx] = mine[...]
-
-    def take(i, carry):
-        @pl.when(i != gx)
-        def _():
-            g_copy(0, i, gy, i).wait_recv()
-
-        @pl.when(not_low)
-        def _():
-            g_copy(1, i, gy, i).wait_recv()
-
-        @pl.when(not_high)
-        def _():
-            g_copy(2, i, gy, i).wait_recv()
-
-        return carry
-
-    lax.fori_loop(0, n, take, 0)
+    g_all(0).wait_recv()
+
+    @pl.when(not_low)
+    def _():
+        g_all(1).wait_recv()
+
+    @pl.when(not_high)
+    def _():
+        g_all(2).wait_recv()
 
     def profile(kind):
         def add(i, total):
@@ -407,12 +427,8 @@
     over = jnp.where(jnp.logical_and(last, not_high), high_raw, over)
     coef_ref[...] = 0.25 * under + 0.5 * raw + 0.25 * over
 
-    def left_x(t, carry):
-        x_copy(0, t).wait_send()
-        x_copy(1, t).wait_send()
-        return carry
-
-    lax.fori_loop(1, nt + 1, left_x, 0)
+    for side in range(2):
+        x_all(side).wait_send()
     for side in range(2):
         c_copy(side).wait_send()
 
@@ -424,25 +440,15 @@
     def _():
         y_copy(1).wait_send()
 
-    def left_g(i, carry):
-        @pl.when(i != gx)
-        def _():
-            g_copy(0, i, gy, gx).wait_send()
-
-        @pl.when(not_low)
-        def _():
-            g_copy(2, i, gy - 1, gx).wait_send()
-
-        @pl.when(not_high)
-        def _():
-            g_copy(1, i, gy + 1, gx).wait_send()
-
-        return carry
-
-    lax.fori_loop(0, n, left_g, 0)
-    inner_out.wait()
-    for copy in rim_out:
-        copy.wait()
+    g_all(0).wait_send()
+
+    @pl.when(not_low)
+    def _():
+        g_all(2).wait_send()
+
+    @pl.when(not_high)
+    def _():
+        g_all(1).wait_send()
 
 
 def local(n, m, velocity):
@@ -456,9 +462,9 @@
             jax.ShapeDtypeStruct((nx, ny, nz), f32),
             jax.ShapeDtypeStruct((1, lanes), f32),
         ),
-        in_specs=[pl.BlockSpec(memory_space=pl.ANY)],
+        in_specs=[pl.BlockSpec(memory_space=pltpu.HBM)],
         out_specs=(
-            pl.BlockSpec(memory_space=pl.ANY),
+            pl.BlockSpec(memory_space=pltpu.VMEM),
             pl.BlockSpec(memory_space=pltpu.VMEM),
         ),
         scratch_shapes=[
@@ -467,29 +473,28 @@
             pltpu.VMEM((3, nx + 4, ny + 16, nz), f32),
             pltpu.VMEM((3, nx + 4, ny + 16, nz), f32),
             pltpu.VMEM((6, nx + 4, ny, nz), f32),
-            pltpu.VMEM((nx, ny, nz), f32),
             pltpu.VMEM((lanes, 128), f32),
             pltpu.VMEM((lanes, 128), f32),
             pltpu.VMEM((2, 16, nz), f32),
             pltpu.VMEM((2, 16, nz), f32),
             pltpu.VMEM((2, lanes), f32),
+            pltpu.VMEM((2, lanes), f32),
             pltpu.VMEM((3, n, 2, lanes), f32),
             pltpu.SemaphoreType.DMA,
-            pltpu.SemaphoreType.DMA((3,)),
-            pltpu.SemaphoreType.DMA((2, nt)),
+            pltpu.SemaphoreType.DMA((2,)),
             pltpu.SemaphoreType.DMA((2, nt)),
             pltpu.SemaphoreType.DMA((2,)),
             pltpu.SemaphoreType.DMA((2,)),
             pltpu.SemaphoreType.DMA((2,)),
             pltpu.SemaphoreType.DMA((2,)),
-            pltpu.SemaphoreType.DMA((3, n)),
-            pltpu.SemaphoreType.DMA((3, n)),
+            pltpu.SemaphoreType.DMA((3,)),
+            pltpu.SemaphoreType.DMA((3,)),
             pltpu.SemaphoreType.REGULAR((n // 2 + 1,)),
         ],
         compiler_params=pltpu.CompilerParams(
-            collective_id=0, has_side_effects=True, vmem_limit_bytes=67043328
+            collective_id=0, has_side_effects=True, vmem_limit_bytes=32 * 1024 * 1024
         ),
-    )(velocity)
+    )(pltpu.with_memory_space_constraint(velocity, pltpu.HBM))
     smooth = coef[0, :ny]
     return (smooth, smooth[None, :, None] * strength)
 

time: 34.7 us -> 32 us (0.922)
  other arithmetic: 1.95 us -> 0.9 us
  Pallas kernels: 31.3 us -> 30.3 us
  local copies, waits for them, and re-layouts: 0.68 us -> 0.01 us
    mul x1, other arithmetic: 1.95 us -> 0.9 us  [local(): return (smooth, smooth[None, :, None] * strength)]
    pallas_call x1, Pallas kernels: 31.3 us -> 30.3 us  [local(): pl.pallas_call(functools.partial(kernel, n, m, nx, ny), out_shape=(jax.Sh...]
    squeeze x1, local copies, waits for them, and re-layouts: 0.67 us -> 0.01 us  [local(): smooth = coef[0, :ny]]
where the time goes in v3:
time: 32 us; the launch traced here: 31.9 us
  Pallas kernels  30.3 us (95%)
  other arithmetic  0.9 us (3%)
  between operations  0.65 us (2%)
    pallas_call x1, Pallas kernels, local(): pl.pallas_call(functools.partial(kernel, n, m, nx, ny), out_shape=(jax.Sh...  30.3 us
    mul x1, other arithmetic, local(): return (smooth, smooth[None, :, None] * strength)  0.9 us

profile of v3, /device:TPU:0, one launch (start us, length us, event | category | flops | bytes accessed | tf_op | source)
XLA Modules:
  0.0 31.9 jit_solution(7201698477197907723)
XLA Ops:
  0.6 30.3 %shard_map.30 = (f32[8,64,256]{2,1,0:T(8,128)S(1)}, f32[1,128]{1,0:T(1,128)S(1)}) custom-call(f32[3,8,64,256]{3,2,1,0:T(8,128)} %u_hbm.1), custom_call_target="tpu_custom_call" | custom-call | tf_op jit(solution)/shard_map/pallas_call | solution.py:459
  30.9 0.0 copy-start
  31.0 0.9 %broadcast_multiply_fusion = f32[8,64,256]{2,1,0:T(8,128)} fusion(f32[8,64,256]{2,1,0:T(8,128)S(1)} %get-tuple-element.5, f32[64]{0:T(128)S(1)} %slice_bitcast_fusion), kind=kLoop, calls=%fused_computation | loop fusion | flops 131072 | bytes 1048832 | tf_op jit(solution)/shard_map/mul | solution.py:499
  31.9 0.0 copy-done
  (1 shorter events, 0.0 us)
Async XLA Ops:
  30.9 0.9 %copy-start = (f32[64]{0:T(128)}, f32[64]{0:T(128)S(1)}, u32[]{:S(2)}) copy-start(f32[64]{0:T(128)S(1)} %slice_bitcast_fusion) | copy-start | bytes 772
